TPU v7x, 32 devices: a whole 2x2x4 slice. The times are simulated.
32 devices in a mesh: cp: 16 (over z, y, x), hd: 2 (over core).
Axes of the slice: x: 2, y: 2, z: 4, core: 2. Of those that a mesh axis runs over, the one named last changes fastest.
Arguments:
- queries: bfloat16 [3072, 4096], P('cp', 'hd'), may hold values from -48 to 48
- keys: bfloat16 [3072, 1024], P('cp', 'hd'), may hold values from -48 to 48
- values: bfloat16 [3072, 1024], P('cp', 'hd'), may hold values from -6 to 6
- span_table: int32 [32], replicated, may hold values from 0 to 31, as said below
- doc_ids: int32 [3072], replicated, may hold values from 0 to 7, never falling along the last dimension, each value on 1 to 768 neighbouring positions
- out_weight: bfloat16 [4096, 4096], P('hd'), may hold values from -0.09375 to 0.09375
Outputs:
- mixed: bfloat16 [3072, 4096], P(('cp', 'hd'))
Inputs may be any that keep to these rules, and one draw needn't show every extreme that they name: `span_table`: slots 2 j and 2 j + 1 hold two spans c and 31 - c, and every span is held once.
All inputs are finite; a program needn't handle non-finite values.
Results may differ from a plain program's by a relative error of at most 0.0095.
Values may be sent and summed in bfloat16 or wider, within the bound.
A program may use at most 128 MiB of HBM per device.

v0:
```python
import jax
import jax.numpy as jnp
from jax import lax
from jax.sharding import PartitionSpec as P

HEAD_WIDTH = 128


def local(queries, keys, values, span_table, doc_ids, out_weight):
    tok_rows = queries.shape[0]
    span_len = tok_rows // 2
    span_count = span_table.shape[0]
    local_heads = queries.shape[1] // HEAD_WIDTH
    kv_heads = keys.shape[1] // HEAD_WIDTH
    query_group = local_heads // kv_heads
    scale = HEAD_WIDTH ** (-0.5)
    slot_onehot = (span_table[:, None] == jnp.arange(span_count, dtype=jnp.int32)[None, :]).astype(
        jnp.float32
    )
    doc_by_span = doc_ids.reshape(span_count, span_len).astype(jnp.float32)
    held_doc = jnp.dot(
        slot_onehot,
        doc_by_span,
        precision=lax.Precision.HIGHEST,
        preferred_element_type=jnp.float32,
    )
    held_doc = held_doc.astype(jnp.int32).reshape(span_count * span_len)
    held_pos = span_table[:, None] * span_len + jnp.arange(span_len, dtype=jnp.int32)[None, :]
    held_pos = held_pos.reshape(span_count * span_len)

    def locate(first):
        place = lax.dynamic_slice_in_dim(held_pos, first, tok_rows, 0)
        document = lax.dynamic_slice_in_dim(held_doc, first, tok_rows, 0)
        return (place, document)

    query_pos, query_doc = locate(lax.axis_index("cp") * tok_rows)
    query_heads = queries.reshape(tok_rows, kv_heads, query_group, HEAD_WIDTH)

    def visit(carry, key_block, value_block, key_start):
        key_pos, key_doc = locate(key_start)
        visible = (key_pos[None, :] <= query_pos[:, None]) & (
            key_doc[None, :] == query_doc[:, None]
        )

        def update(state):
            best, total, accum = state
            key_head_rows = key_block.reshape(tok_rows, kv_heads, HEAD_WIDTH)
            value_head_rows = value_block.reshape(tok_rows, kv_heads, HEAD_WIDTH)
            scores = (
                jnp.einsum(
                    "qkgd,nkd->kgqn", query_heads, key_head_rows, preferred_element_type=jnp.float32
                )
                * scale
            )
            scores = jnp.where(visible, scores, -1e30)
            new_best = jnp.maximum(best, jnp.max(scores, axis=-1))
            weights = jnp.where(visible, jnp.exp(scores - new_best[..., None]), 0.0)
            fade = jnp.exp(best - new_best)
            total = total * fade + jnp.sum(weights, axis=-1)
            accum = accum * fade[..., None] + jnp.einsum(
                "kgqn,nkd->kgqd",
                weights.astype(jnp.bfloat16),
                value_head_rows,
                preferred_element_type=jnp.float32,
            )
            return (new_best, total, accum)

        return lax.cond(jnp.any(visible), update, lambda state: state, carry)

    init = (
        jnp.full((kv_heads, query_group, tok_rows), -1e30, jnp.float32),
        jnp.zeros((kv_heads, query_group, tok_rows), jnp.float32),
        jnp.zeros((kv_heads, query_group, tok_rows, HEAD_WIDTH), jnp.float32),
    )
    key_piece = lax.all_gather(keys, "cp", axis=0, tiled=True)
    value_piece = lax.all_gather(values, "cp", axis=0, tiled=True)
    count = key_piece.shape[0] // tok_rows

    def step(index, state):
        offset = (index * tok_rows).astype(jnp.int32)
        key_block = lax.dynamic_slice_in_dim(key_piece, offset, tok_rows, 0)
        value_block = lax.dynamic_slice_in_dim(value_piece, offset, tok_rows, 0)
        return visit(state, key_block, value_block, offset)

    best, total, accum = lax.fori_loop(0, count, step, init)
    attn = (
        (accum / total[..., None])
        .transpose(2, 0, 1, 3)
        .reshape(tok_rows, local_heads * HEAD_WIDTH)
        .astype(jnp.bfloat16)
    )
    return lax.psum_scatter(
        jnp.dot(attn, out_weight, preferred_element_type=jnp.float32).astype(jnp.bfloat16),
        "hd",
        scatter_dimension=0,
        tiled=True,
    )


def solution(mesh):
    return jax.shard_map(
        local,
        mesh=mesh,
        in_specs=(P("cp", "hd"), P("cp", "hd"), P("cp", "hd"), P(), P(), P("hd", None)),
        out_specs=P(("cp", "hd"), None),
        check_vma=False,
    )
```

profile of v0, /device:TPU:0, one launch (start us, length us, event | category | flops | bytes accessed | tf_op | source)
XLA Modules:
  0.0 244.5 jit_solution(14145306607009826491)
XLA Ops:
  10.7 2.3 reshape.35
  13.2 67.5 %all-gather.3.cloned.1.call-done = bf16[3072,512]{1,0:T(8,128)(2,1)} async-done(((bf16[192,512]{1,0:T(8,128)(2,1)}), bf16[3072,512]{1,0:T(8,128)(2,1)}) %all-gather.3.cloned.1.call-update) | async-done | bytes 3145744 | tf_op jit(solution)/shard_map/all_gather | solution.py:75
  80.7 69.2 %all-gather.5.cloned.1.call-done = bf16[3072,512]{1,0:T(8,128)(2,1)} async-done(((bf16[192,512]{1,0:T(8,128)(2,1)}), bf16[3072,512]{1,0:T(8,128)(2,1)}) %all-gather.5.cloned.1.call-update) | async-done | bytes 3145744 | tf_op jit(solution)/shard_map/all_gather | solution.py:76
  150.1 68.0 %while.17 = (s32[]{:T(128)}, f32[4,4,192]{2,1,0:T(4,128)S(1)}, f32[4,4,192]{2,1,0:T(4,128)S(1)}, f32[4,4,192,128]{3,2,1,0:T(8,128)S(1)}, s32[3072]{0:T(1024)S(1)...) while((s32[]{:T(128)}, f32[4,4,192]{2,1,0:T(4,128)S(1)}, ...), condition=%wide.region_6.7_spmd, body=%wide.region_0.6_spmd.sunk | while | flops 310597632 | bytes 13326661 | solution.py:85
  151.6 4.4 %conditional.2 = ((f32[4,4,192]{2,1,0:T(4,128)S(1)}, f32[4,4,192]{2,1,0:T(4,128)S(1)}, f32[4,4,192,128]{3,2,1,0:T(8,128)S(1)})) conditional(s32[]{:T(128)} %convert_element_type.51, (f32[4,4,192]{2,1,0:T(4,128)S(1)}, f32[4,4,192]{2,1,0:T(4,128)S(1)}, f32[4,4,192,128]{3,2,1,0:T(8,128)S(1)}) %tuple.49, (pred[192,192]{0,1:T(8,128)(4,1)S(1)}, ...), branch_computations={%region_2.0_spmd, %region_3.5_spmd} | conditional | flops 310450176 | bytes 13283364 | solution.py:68
  159.0 4.4 %conditional.2 = ((f32[4,4,192]{2,1,0:T(4,128)S(1)}, f32[4,4,192]{2,1,0:T(4,128)S(1)}, f32[4,4,192,128]{3,2,1,0:T(8,128)S(1)})) conditional(s32[]{:T(128)} %convert_element_type.51, (f32[4,4,192]{2,1,0:T(4,128)S(1)}, f32[4,4,192]{2,1,0:T(4,128)S(1)}, f32[4,4,192,128]{3,2,1,0:T(8,128)S(1)}) %tuple.49, (pred[192,192]{0,1:T(8,128)(4,1)S(1)}, ...), branch_computations={%region_2.0_spmd, %region_3.5_spmd} | conditional | flops 310450176 | bytes 13283364 | solution.py:68
  161.7 1.6 multiply_add_fusion
  166.3 4.4 %conditional.2 = ((f32[4,4,192]{2,1,0:T(4,128)S(1)}, f32[4,4,192]{2,1,0:T(4,128)S(1)}, f32[4,4,192,128]{3,2,1,0:T(8,128)S(1)})) conditional(s32[]{:T(128)} %convert_element_type.51, (f32[4,4,192]{2,1,0:T(4,128)S(1)}, f32[4,4,192]{2,1,0:T(4,128)S(1)}, f32[4,4,192,128]{3,2,1,0:T(8,128)S(1)}) %tuple.49, (pred[192,192]{0,1:T(8,128)(4,1)S(1)}, ...), branch_computations={%region_2.0_spmd, %region_3.5_spmd} | conditional | flops 310450176 | bytes 13283364 | solution.py:68
  169.1 1.6 multiply_add_fusion
  172.3 4.4 %conditional.2 = ((f32[4,4,192]{2,1,0:T(4,128)S(1)}, f32[4,4,192]{2,1,0:T(4,128)S(1)}, f32[4,4,192,128]{3,2,1,0:T(8,128)S(1)})) conditional(s32[]{:T(128)} %convert_element_type.51, (f32[4,4,192]{2,1,0:T(4,128)S(1)}, f32[4,4,192]{2,1,0:T(4,128)S(1)}, f32[4,4,192,128]{3,2,1,0:T(8,128)S(1)}) %tuple.49, (pred[192,192]{0,1:T(8,128)(4,1)S(1)}, ...), branch_computations={%region_2.0_spmd, %region_3.5_spmd} | conditional | flops 310450176 | bytes 13283364 | solution.py:68
  175.1 1.6 multiply_add_fusion
  179.7 4.4 %conditional.2 = ((f32[4,4,192]{2,1,0:T(4,128)S(1)}, f32[4,4,192]{2,1,0:T(4,128)S(1)}, f32[4,4,192,128]{3,2,1,0:T(8,128)S(1)})) conditional(s32[]{:T(128)} %convert_element_type.51, (f32[4,4,192]{2,1,0:T(4,128)S(1)}, f32[4,4,192]{2,1,0:T(4,128)S(1)}, f32[4,4,192,128]{3,2,1,0:T(8,128)S(1)}) %tuple.49, (pred[192,192]{0,1:T(8,128)(4,1)S(1)}, ...), branch_computations={%region_2.0_spmd, %region_3.5_spmd} | conditional | flops 310450176 | bytes 13283364 | solution.py:68
  188.5 4.4 %conditional.2 = ((f32[4,4,192]{2,1,0:T(4,128)S(1)}, f32[4,4,192]{2,1,0:T(4,128)S(1)}, f32[4,4,192,128]{3,2,1,0:T(8,128)S(1)})) conditional(s32[]{:T(128)} %convert_element_type.51, (f32[4,4,192]{2,1,0:T(4,128)S(1)}, f32[4,4,192]{2,1,0:T(4,128)S(1)}, f32[4,4,192,128]{3,2,1,0:T(8,128)S(1)}) %tuple.49, (pred[192,192]{0,1:T(8,128)(4,1)S(1)}, ...), branch_computations={%region_2.0_spmd, %region_3.5_spmd} | conditional | flops 310450176 | bytes 13283364 | solution.py:68
  191.3 1.6 multiply_add_fusion
  194.4 4.4 %conditional.2 = ((f32[4,4,192]{2,1,0:T(4,128)S(1)}, f32[4,4,192]{2,1,0:T(4,128)S(1)}, f32[4,4,192,128]{3,2,1,0:T(8,128)S(1)})) conditional(s32[]{:T(128)} %convert_element_type.51, (f32[4,4,192]{2,1,0:T(4,128)S(1)}, f32[4,4,192]{2,1,0:T(4,128)S(1)}, f32[4,4,192,128]{3,2,1,0:T(8,128)S(1)}) %tuple.49, (pred[192,192]{0,1:T(8,128)(4,1)S(1)}, ...), branch_computations={%region_2.0_spmd, %region_3.5_spmd} | conditional | flops 310450176 | bytes 13283364 | solution.py:68
  197.2 1.6 multiply_add_fusion
  200.3 4.4 %conditional.2 = ((f32[4,4,192]{2,1,0:T(4,128)S(1)}, f32[4,4,192]{2,1,0:T(4,128)S(1)}, f32[4,4,192,128]{3,2,1,0:T(8,128)S(1)})) conditional(s32[]{:T(128)} %convert_element_type.51, (f32[4,4,192]{2,1,0:T(4,128)S(1)}, f32[4,4,192]{2,1,0:T(4,128)S(1)}, f32[4,4,192,128]{3,2,1,0:T(8,128)S(1)}) %tuple.49, (pred[192,192]{0,1:T(8,128)(4,1)S(1)}, ...), branch_computations={%region_2.0_spmd, %region_3.5_spmd} | conditional | flops 310450176 | bytes 13283364 | solution.py:68
  203.1 1.6 multiply_add_fusion
  206.3 4.4 %conditional.2 = ((f32[4,4,192]{2,1,0:T(4,128)S(1)}, f32[4,4,192]{2,1,0:T(4,128)S(1)}, f32[4,4,192,128]{3,2,1,0:T(8,128)S(1)})) conditional(s32[]{:T(128)} %convert_element_type.51, (f32[4,4,192]{2,1,0:T(4,128)S(1)}, f32[4,4,192]{2,1,0:T(4,128)S(1)}, f32[4,4,192,128]{3,2,1,0:T(8,128)S(1)}) %tuple.49, (pred[192,192]{0,1:T(8,128)(4,1)S(1)}, ...), branch_computations={%region_2.0_spmd, %region_3.5_spmd} | conditional | flops 310450176 | bytes 13283364 | solution.py:68
  209.1 1.6 multiply_add_fusion
  213.7 4.4 %conditional.2 = ((f32[4,4,192]{2,1,0:T(4,128)S(1)}, f32[4,4,192]{2,1,0:T(4,128)S(1)}, f32[4,4,192,128]{3,2,1,0:T(8,128)S(1)})) conditional(s32[]{:T(128)} %convert_element_type.51, (f32[4,4,192]{2,1,0:T(4,128)S(1)}, f32[4,4,192]{2,1,0:T(4,128)S(1)}, f32[4,4,192,128]{3,2,1,0:T(8,128)S(1)}) %tuple.49, (pred[192,192]{0,1:T(8,128)(4,1)S(1)}, ...), branch_computations={%region_2.0_spmd, %region_3.5_spmd} | conditional | flops 310450176 | bytes 13283364 | solution.py:68
  216.4 1.6 multiply_add_fusion
  219.8 10.4 %convolution_convert_fusion = bf16[192,4096]{1,0:T(8,128)(2,1)} fusion(bf16[192,2048]{1,0:T(8,128)(2,1)S(1)} %convert_element_type.39, bf16[2048,4096]{1,0:T(8,128)(2,1)} %param.15), kind=kOutput, calls=%fused_computation.23 | convolution fusion | flops 3222011904 | bytes 19136512 | tf_op jit(solution)/shard_map/dot_general | solution.py:93
  230.2 7.7 %reduce-scatter.2.cloned.1.call-done = bf16[96,4096]{1,0:T(8,128)(2,1)} async-done(((bf16[192,4096]{1,0:T(8,128)(2,1)}), bf16[96,4096]{1,0:T(8,128)(2,1)}) %reduce-scatter.2.cloned.1.call-update) | async-done | bytes 786448 | tf_op jit(solution)/shard_map/reduce_scatter | solution.py:92
  (158 shorter events, 51.2 us)
Async XLA Ops:
  6.5 74.2 %all-gather.3.cloned.1.call-start = ((), (), s32[]{:S(2)}) async-start(), calls=%async_computation.1 | async-start | bytes 3342336 | tf_op jit(solution)/shard_map/all_gather | solution.py:75
  7.3 142.7 %all-gather.5.cloned.1.call-start = ((), (), s32[]{:S(2)}) async-start(), calls=%async_computation.2 | async-start | bytes 3342336 | tf_op jit(solution)/shard_map/all_gather | solution.py:76
  8.0 229.9 %reduce-scatter.2.cloned.1.call-start = ((), (), s32[]{:S(2)}) async-start(), calls=%async_computation.3 | async-start | bytes 2359296 | tf_op jit(solution)/shard_map/reduce_scatter | solution.py:92
Sparse Core Ops, SparseCore 0:
  10.1 70.5 all-gather.2
  83.5 66.3 all-gather.4
  230.3 7.5 reduce-scatter.1
where the time goes:
time: 245 us; the launch traced here: 244 us
  waiting for transfers between devices  146 us (60%)
  matrix products  34.9 us (14%)
  other arithmetic  22.1 us (9%)
  local copies, waits for them, and re-layouts  18.3 us (7%)
  between operations  13.2 us (5%)
  loops' own time  10 us (4%)
    all_gather x1, waiting for transfers between devices, local(): value_piece = lax.all_gather(values, 'cp', axis=0, tiled=True)  69.2 us
    all_gather x1, waiting for transfers between devices, local(): key_piece = lax.all_gather(keys, 'cp', axis=0, tiled=True)  67.5 us
    dot_general x10, matrix products, update(): jnp.einsum('kgqn,nkd->kgqd', weights.astype(jnp.bfloat16), value_head_row...  16.3 us
    reduce_or x16, other arithmetic, visit(): return lax.cond(jnp.any(visible), update, lambda state: state, carry)  11.6 us
    dynamic_slice x10, local copies, waits for them, and re-layouts, step(): value_block = lax.dynamic_slice_in_dim(value_piece, offset, tok_rows, 0)  10.6 us
    dot_general x1, matrix products, local(): jnp.dot(attn, out_weight, preferred_element_type=jnp.float32)  10.4 us
    another operation x1, loops' own time, local(): best, total, accum = lax.fori_loop(0, count, step, init)  9.39 us
    reduce_sum x10, other arithmetic, update(): total = total * fade + jnp.sum(weights, axis=-1)  8.35 us
  transfers between devices with their start and end apart: 3, of which 3 were waited for; matrix products, arithmetic and copies ran while one was open for 2% of the time, Pallas kernels for 0%

commit v1 on v0

v1 whole, which is shorter than its diff:
```python
import functools
import math

import jax
import jax.numpy as jnp
from jax import lax
from jax.experimental import pallas as pl
from jax.experimental.pallas import tpu as pltpu
from jax.sharding import PartitionSpec as P

HEAD_WIDTH = 128
DOCS = 8
LANES = 256
NEG = -1e30
MESH = pl.DeviceIdType.MESH


def kernel(
    line, q_ref, span_ref, doc_ref, k_hbm, v_hbm, w_hbm, out_ref,
    kv, w_vmem, q_t, acc, best, total, bias, low, high, attn, outgoing, incoming, kept,
    load_sem, w_sem, send0, send_z, send_xy, recv, out_send, out_recv,
):
    rows = q_ref.shape[0]
    span_len = rows // 2
    kv_heads = k_hbm.shape[1] // HEAD_WIDTH
    group = q_ref.shape[1] // HEAD_WIDTH // kv_heads
    tiles = group * rows // LANES
    third, sixth = rows // 3, rows // 6
    me = lax.axis_index("cp")
    hd = lax.axis_index("hd")
    z = me // 4
    y = (me // 2) % 2
    x = me % 2

    def slot(zz, fx, fy):
        xx = 1 - x if fx else x
        yy = 1 - y if fy else y
        return zz * 4 + yy * 2 + xx

    piece_rows = {
        "A": (0, third, 0), "B": (third, third, 1), "C": (2 * third, third, 2),
        "C0": (2 * third, sixth, 2), "C1": (2 * third + sixth, sixth, 3),
    }

    def part(src, piece):
        start, size, _ = piece_rows[piece]
        return kv.at[src, :, pl.ds(start, size), :]

    def copy_of(src, piece, target, sem):
        return pltpu.make_async_remote_copy(
            src_ref=part(src, piece), dst_ref=part(src, piece), send_sem=sem,
            recv_sem=recv.at[src, piece_rows[piece][2]],
            device_id={"cp": target}, device_id_type=MESH,
        )

    def arrived(src, piece):
        copy_of(src, piece, slot(z, True, False), send0.at[0]).wait_recv()

    to_x, to_y = slot(z, True, False), slot(z, False, True)
    up, down = me + 4, me - 4
    has_up, has_down = z < line - 1, z > 0

    loads = [
        pltpu.make_async_copy(k_hbm, kv.at[me, 0], load_sem.at[0]),
        pltpu.make_async_copy(v_hbm, kv.at[me, 1], load_sem.at[1]),
    ]
    w_load = pltpu.make_async_copy(w_hbm, w_vmem, w_sem)
    for load in loads:
        load.start()
    barrier = pltpu.get_barrier_semaphore()
    for target in (to_x, to_y):
        pl.semaphore_signal(barrier, inc=1, device_id={"cp": target}, device_id_type=MESH)
    pl.semaphore_signal(barrier, inc=1, device_id={"hd": 1 - hd}, device_id_type=MESH)

    @pl.when(has_up)
    def _():
        pl.semaphore_signal(barrier, inc=1, device_id={"cp": up}, device_id_type=MESH)

    @pl.when(has_down)
    def _():
        pl.semaphore_signal(barrier, inc=1, device_id={"cp": down}, device_id_type=MESH)

    pl.semaphore_wait(barrier, 3 + has_up.astype(jnp.int32) + has_down.astype(jnp.int32))
    for load in loads:
        load.wait()

    own, xn, yn, dg = (False, False), (True, False), (False, True), (True, True)
    first_x = [(own, "A"), (own, "C"), (own, "B")]
    first_y = [(own, "B"), (own, "C"), (own, "A")]
    first_z = [(own, "C"), (own, "A"), (own, "B")]
    later_z = [(xn, "A"), (yn, "B")]

    def first_stage(act, xs, ys, zs, nx, ny, nz):
        for i in range(max(len(xs), len(ys))):
            if i < len(xs):
                act(copy_of(slot(z, *xs[i][0]), xs[i][1], to_x, send0.at[nx + i]))
            if i < len(ys):
                act(copy_of(slot(z, *ys[i][0]), ys[i][1], to_y, send0.at[5 + ny + i]))

        @pl.when(has_up)
        def _():
            for i, (flips, piece) in enumerate(zs):
                act(copy_of(slot(z, *flips), piece, up, send0.at[10 + nz + i]))

        @pl.when(has_down)
        def _():
            for i, (flips, piece) in enumerate(zs):
                act(copy_of(slot(z, *flips), piece, down, send0.at[15 + nz + i]))

    def go(copy):
        copy.start()

    def sent(copy):
        copy.wait_send()

    first_stage(go, first_x, first_y, first_z, 0, 0, 0)
    w_load.start()

    lane = lax.broadcasted_iota(jnp.int32, (1, tiles * LANES), 1) % rows
    span0, span1 = span_ref[2 * me], span_ref[2 * me + 1]
    row_pos = jnp.where(lane < span_len, span0 * span_len + lane, (span1 - 1) * span_len + lane)
    row_pos = row_pos.astype(jnp.float32)
    row_low = jnp.zeros_like(row_pos)
    docs = doc_ref[...]
    for d in range(1, DOCS):
        start = jnp.sum(jnp.where(docs < d, 1.0, 0.0), keepdims=True)
        row_low = jnp.maximum(row_low, jnp.where(start <= row_pos, start, 0.0))
    for c in range(tiles):
        low[c] = row_low[:, c * LANES:(c + 1) * LANES]
        high[c] = row_pos[:, c * LANES:(c + 1) * LANES]
    for g in range(kv_heads):
        heads = [q_ref[:, (g * group + h) * HEAD_WIDTH:(g * group + h + 1) * HEAD_WIDTH] for h in range(group)]
        flipped = jnp.concatenate(heads, axis=0).T
        for c in range(tiles):
            q_t[g, c] = flipped[:, c * LANES:(c + 1) * LANES]

    factor = HEAD_WIDTH ** (-0.5) * math.log2(math.e)

    def attend(src, initial=False):
        s0, s1 = span_ref[2 * src], span_ref[2 * src + 1]
        key = lax.broadcasted_iota(jnp.int32, (rows, LANES), 0)
        key_pos = jnp.where(key < span_len, s0 * span_len, (s1 - 1) * span_len) + key
        key_pos = key_pos.astype(jnp.float32)
        for c in range(tiles):
            visible = (key_pos >= low[c]) & (key_pos <= high[c])
            bias[c] = jnp.where(visible, 0.0, NEG)

        @pl.loop(0, kv_heads)
        def _(g):
            columns = pl.ds(pl.multiple_of(g * HEAD_WIDTH, HEAD_WIDTH), HEAD_WIDTH)
            keys = kv[src, 0, :, columns]
            values = kv[src, 1, :, columns]
            for c in range(tiles):
                scores = jnp.dot(keys, q_t[g, c], preferred_element_type=jnp.float32)
                scores = scores * factor + bias[c]
                top = jnp.max(scores, axis=0, keepdims=True)
                if not initial:
                    old = best[g, c]
                    top = jnp.maximum(old, top)
                    fade = jnp.exp2(old - top)
                weights = jnp.exp2(scores - top)
                weight_sum = jnp.sum(weights, axis=0, keepdims=True)
                part_sum = lax.dot_general(
                    values, weights.astype(jnp.bfloat16), (((0,), (0,)), ((), ())),
                    preferred_element_type=jnp.float32,
                )
                best[g, c] = top
                if initial:
                    total[g, c] = weight_sum
                    acc[g, c] = part_sum
                else:
                    total[g, c] = total[g, c] * fade + weight_sum
                    acc[g, c] = acc[g, c] * fade + part_sum

    attend(me, initial=True)

    arrived(slot(z, *xn), "A")
    arrived(slot(z, *yn), "B")
    first_stage(go, [(yn, "B")], [(xn, "A")], later_z, 3, 3, 3)
    arrived(slot(z, *xn), "C")
    arrived(slot(z, *yn), "C")
    first_stage(go, [(yn, "C0")], [(xn, "C1")], [], 4, 4, 0)
    arrived(slot(z, *xn), "B")
    attend(slot(z, *xn))
    arrived(slot(z, *yn), "A")
    attend(slot(z, *yn))

    near = jnp.minimum(z, line - 1 - z)

    def plane(j):
        both = jnp.where(j % 2 == 1, z + (j + 1) // 2, z - j // 2)
        rest = jnp.where(z < line - 1 - z, j, line - 1 - j)
        return jnp.where(j <= 2 * near, both, rest)

    def sides(i, fn):
        @pl.when(z - i >= 0)
        def _():
            fn(z - i, 0, has_up, up)

        @pl.when(z + i < line)
        def _():
            fn(z + i, 1, has_down, down)

    z_pieces = [(own, "C", "xy"), (own, "A", "y"), (own, "B", "x"), (xn, "A", "y"), (yn, "B", "x")]

    def z_step(i, n, act):
        flips, piece, links = z_pieces[n]

        def fn(zz, side, can, target):
            src = slot(zz, *flips)
            if act is go:
                arrived(src, piece)

            @pl.when(can)
            def _():
                act(copy_of(src, piece, target, send_z.at[i - 1, side, n]))

            if "x" in links:
                act(copy_of(src, piece, to_x, send_xy.at[i - 1, side, 0, min(n, 2)
                                                         if n != 4 else 1]))
            if "y" in links:
                act(copy_of(src, piece, to_y, send_xy.at[i - 1, side, 1, min(n, 2)]))

        sides(i, fn)

    def corner_step(i, act):
        def fn(zz, side, can, target):
            src_x, src_y = slot(zz, *xn), slot(zz, *yn)
            if act is go:
                arrived(src_x, "C")
            act(copy_of(src_x, "C1", to_y, send_xy.at[i - 1, side, 1, 3]))
            if act is go:
                arrived(src_y, "C")
            act(copy_of(src_y, "C0", to_x, send_xy.at[i - 1, side, 0, 3]))

        sides(i, fn)

    def wait_step(i, flips, pieces):
        def fn(zz, side, can, target):
            for piece in pieces:
                arrived(slot(zz, *flips), piece)

        sides(i, fn)

    dg_pieces = ("B", "A", "C0", "C1")

    for piece in dg_pieces:
        arrived(slot(z, *dg), piece)
    attend(slot(z, *dg))

    def stage(i, carry):
        for n in range(3):
            z_step(i, n, go)
        here = plane(i)
        attend(slot(here, *own))
        z_step(i, 3, go)
        z_step(i, 4, go)
        corner_step(i, go)
        wait_step(i, xn, ("B",))
        attend(slot(here, *xn))
        wait_step(i, yn, ("A",))
        attend(slot(here, *yn))
        wait_step(i, dg, dg_pieces)
        attend(slot(here, *dg))
        return carry

    lax.fori_loop(1, line, stage, 0)

    for g in range(kv_heads):
        parts = [acc[g, c] / total[g, c] for c in range(tiles)]
        turned = jnp.concatenate(parts, axis=1).T.astype(jnp.bfloat16)
        for h in range(group):
            first = (g * group + h) * HEAD_WIDTH
            attn[:, first:first + HEAD_WIDTH] = turned[h * rows:(h + 1) * rows]

    w_load.wait()
    half = rows // 2
    count, width = outgoing.shape[0], outgoing.shape[2]

    def hand_over(n):
        return pltpu.make_async_remote_copy(
            src_ref=outgoing.at[n], dst_ref=incoming.at[n], send_sem=out_send.at[n],
            recv_sem=out_recv.at[n], device_id={"hd": 1 - hd}, device_id_type=MESH,
        )

    @pl.loop(0, count)
    def _(n):
        columns = pl.ds(pl.multiple_of(n * width, width), width)
        product = jnp.dot(attn[...], w_vmem[:, columns], preferred_element_type=jnp.float32)
        upper, lower = product[:half], product[half:]
        mine = hd == 0
        outgoing[n] = jnp.where(mine, lower, upper).astype(jnp.bfloat16)
        kept[n] = jnp.where(mine, upper, lower)
        hand_over(n).start()

    for n in range(count):
        hand_over(n).wait_recv()
        out_ref[:, n * width:(n + 1) * width] = (kept[n] + incoming[n].astype(jnp.float32)).astype(jnp.bfloat16)

    for n in range(count):
        hand_over(n).wait_send()
    first_stage(sent, first_x, first_y, first_z, 0, 0, 0)
    first_stage(sent, [(yn, "B")], [(xn, "A")], later_z, 3, 3, 3)
    first_stage(sent, [(yn, "C0")], [(xn, "C1")], [], 4, 4, 0)

    def drain(i, carry):
        for n in range(5):
            z_step(i, n, sent)
        corner_step(i, sent)
        return carry

    lax.fori_loop(1, line, drain, 0)


def local(cp, queries, keys, values, span_table, doc_ids, out_weight):
    rows = queries.shape[0]
    kv_heads = keys.shape[1] // HEAD_WIDTH
    group = queries.shape[1] // HEAD_WIDTH // kv_heads
    tiles = group * rows // LANES
    line = cp // 4
    model = out_weight.shape[1]
    count = 8
    width = model // count
    half = rows // 2
    vmem, hbm = pltpu.VMEM, pl.ANY
    spec = lambda space: pl.BlockSpec(memory_space=space)
    dma = pltpu.SemaphoreType.DMA
    f32, bf16 = jnp.float32, jnp.bfloat16
    return pl.pallas_call(
        functools.partial(kernel, line),
        out_shape=jax.ShapeDtypeStruct((half, model), bf16),
        in_specs=[spec(vmem), spec(pltpu.SMEM), spec(vmem), spec(hbm), spec(hbm), spec(hbm)],
        out_specs=spec(vmem),
        scratch_shapes=[
            vmem((cp, 2, rows, keys.shape[1]), bf16),
            vmem(out_weight.shape, bf16),
            vmem((kv_heads, tiles, HEAD_WIDTH, LANES), bf16),
            vmem((kv_heads, tiles, HEAD_WIDTH, LANES), f32),
            vmem((kv_heads, tiles, 1, LANES), f32),
            vmem((kv_heads, tiles, 1, LANES), f32),
            vmem((tiles, rows, LANES), f32),
            vmem((tiles, 1, LANES), f32),
            vmem((tiles, 1, LANES), f32),
            vmem((rows, queries.shape[1]), bf16),
            vmem((count, half, width), bf16),
            vmem((count, half, width), bf16),
            vmem((count, half, width), f32),
            dma((2,)), dma, dma((20,)), dma((line, 2, 5)), dma((line, 2, 2, 4)),
            dma((cp, 4)), dma((count,)), dma((count,)),
        ],
        compiler_params=pltpu.CompilerParams(
            collective_id=0, has_side_effects=True, vmem_limit_bytes=60 * 2 ** 20,
        ),
    )(queries, span_table, doc_ids.reshape(-1, 128), keys, values, out_weight)


def solution(mesh):
    return jax.shard_map(
        functools.partial(local, mesh.shape["cp"]),
        mesh=mesh,
        in_specs=(P("cp", "hd"), P("cp", "hd"), P("cp", "hd"), P(), P(), P("hd", None)),
        out_specs=P(("cp", "hd"), None),
        check_vma=False,
    )
```

time: 245 us -> 93 us (0.38)
  the two profiles are of different devices: /device:TPU:0 before, /device:TPU:9 now
where the time goes in v1:
time: 93 us; the launch traced here: 92.8 us
  Pallas kernels  90.7 us (98%)
  local copies, waits for them, and re-layouts  2.06 us (2%)
    pallas_call x1, Pallas kernels, local(): pl.pallas_call(functools.partial(kernel, line), out_shape=jax.ShapeDtypeS...  90.7 us
    unnamed x1, local copies, waits for them, and re-layouts  2.06 us

profile of v1, /device:TPU:9, one launch (start us, length us, event | category | flops | bytes accessed | tf_op | source)
XLA Modules:
  0.0 92.8 jit_solution(12314457596242711454)
XLA Ops:
  0.0 90.7 %shard_map.64 = bf16[96,4096]{1,0:T(8,128)(2,1)} custom-call(bf16[192,2048]{1,0:T(8,128)(2,1)} %q_ref.1, s32[32]{0:T(128)} %span_ref.1, s32[24,128]{1,0:T(8,128)} %bitcast.1, bf16[192,512]{1,0:T(8,128)(2,1)} %k_hbm.1, bf16[192,512]{1,0:T(8,128)(2,1)} %v_hbm.1, bf16[2048,4096]{1,0:T(8,128)(2,1)} %w_hbm.1), custom_call_target="tpu_custom_call" | custom-call | tf_op jit(solution)/shard_map/pallas_call | solution.py:329
  90.7 2.1 %copy.8 = bf16[96,4096]{1,0:T(8,128)(2,1)} copy(bf16[96,4096]{1,0:T(8,128)(2,1)} %shard_map.64) | data formatting | bytes 1572864

commit v2 on v1

--- a/solution.py
+++ b/solution.py
@@ -17,7 +17,7 @@
 
 def kernel(
     line, q_ref, span_ref, doc_ref, k_hbm, v_hbm, w_hbm, out_ref,
-    kv, w_vmem, q_t, acc, best, total, bias, low, high, attn, outgoing, incoming, kept,
+    kv, w_vmem, q_t, acc, best, total, fades, held, bias, low, high, attn, outgoing, incoming, kept,
     load_sem, w_sem, send0, send_z, send_xy, recv, out_send, out_recv,
 ):
     rows = q_ref.shape[0]
@@ -145,11 +145,8 @@
             visible = (key_pos >= low[c]) & (key_pos <= high[c])
             bias[c] = jnp.where(visible, 0.0, NEG)
 
-        @pl.loop(0, kv_heads)
-        def _(g):
-            columns = pl.ds(pl.multiple_of(g * HEAD_WIDTH, HEAD_WIDTH), HEAD_WIDTH)
-            keys = kv[src, 0, :, columns]
-            values = kv[src, 1, :, columns]
+        def weigh(g):
+            keys = kv[src, 0, :, g * HEAD_WIDTH:(g + 1) * HEAD_WIDTH]
             for c in range(tiles):
                 scores = jnp.dot(keys, q_t[g, c], preferred_element_type=jnp.float32)
                 scores = scores * factor + bias[c]
@@ -158,19 +155,24 @@
                     old = best[g, c]
                     top = jnp.maximum(old, top)
                     fade = jnp.exp2(old - top)
+                    fades[g, c] = fade
                 weights = jnp.exp2(scores - top)
                 weight_sum = jnp.sum(weights, axis=0, keepdims=True)
-                part_sum = lax.dot_general(
-                    values, weights.astype(jnp.bfloat16), (((0,), (0,)), ((), ())),
-                    preferred_element_type=jnp.float32,
-                )
                 best[g, c] = top
-                if initial:
-                    total[g, c] = weight_sum
-                    acc[g, c] = part_sum
-                else:
-                    total[g, c] = total[g, c] * fade + weight_sum
-                    acc[g, c] = acc[g, c] * fade + part_sum
+                total[g, c] = weight_sum if initial else total[g, c] * fade + weight_sum
+                held[g, c] = weights.astype(jnp.bfloat16)
+
+        def gather(g):
+            values = kv[src, 1, :, g * HEAD_WIDTH:(g + 1) * HEAD_WIDTH].T
+            for c in range(tiles):
+                part_sum = jnp.dot(values, held[g, c], preferred_element_type=jnp.float32)
+                acc[g, c] = part_sum if initial else acc[g, c] * fades[g, c] + part_sum
+
+        for g in range(kv_heads):
+            weigh(g)
+            if g:
+                gather(g - 1)
+        gather(kv_heads - 1)
 
     attend(me, initial=True)
 
@@ -338,6 +340,8 @@
             vmem((kv_heads, tiles, HEAD_WIDTH, LANES), f32),
             vmem((kv_heads, tiles, 1, LANES), f32),
             vmem((kv_heads, tiles, 1, LANES), f32),
+            vmem((kv_heads, tiles, 1, LANES), f32),
+            vmem((kv_heads, tiles, rows, LANES), bf16),
             vmem((tiles, rows, LANES), f32),
             vmem((tiles, 1, LANES), f32),
             vmem((tiles, 1, LANES), f32),

time: 93 us -> 73.7 us (0.79)
  the two profiles are of different devices: /device:TPU:9 before, /device:TPU:0 now
where the time goes in v2:
time: 73.7 us; the launch traced here: 73.5 us
  Pallas kernels  71.5 us (97%)
  local copies, waits for them, and re-layouts  2.06 us (3%)
    pallas_call x1, Pallas kernels, local(): pl.pallas_call(functools.partial(kernel, line), out_shape=jax.ShapeDtypeS...  71.5 us
    unnamed x1, local copies, waits for them, and re-layouts  2.06 us

profile of v2, /device:TPU:0, one launch (start us, length us, event | category | flops | bytes accessed | tf_op | source)
XLA Modules:
  0.0 73.5 jit_solution(6660627486172517887)
XLA Ops:
  0.0 71.5 %shard_map.64 = bf16[96,4096]{1,0:T(8,128)(2,1)} custom-call(bf16[192,2048]{1,0:T(8,128)(2,1)} %q_ref.1, s32[32]{0:T(128)} %span_ref.1, s32[24,128]{1,0:T(8,128)} %bitcast.1, bf16[192,512]{1,0:T(8,128)(2,1)} %k_hbm.1, bf16[192,512]{1,0:T(8,128)(2,1)} %v_hbm.1, bf16[2048,4096]{1,0:T(8,128)(2,1)} %w_hbm.1), custom_call_target="tpu_custom_call" | custom-call | tf_op jit(solution)/shard_map/pallas_call | solution.py:331
  71.5 2.1 %copy.8 = bf16[96,4096]{1,0:T(8,128)(2,1)} copy(bf16[96,4096]{1,0:T(8,128)(2,1)} %shard_map.64) | data formatting | bytes 1572864

commit v3 on v2

--- a/solution.py
+++ b/solution.py
@@ -25,7 +25,8 @@
     kv_heads = k_hbm.shape[1] // HEAD_WIDTH
     group = q_ref.shape[1] // HEAD_WIDTH // kv_heads
     tiles = group * rows // LANES
-    third, sixth = rows // 3, rows // 6
+    whole = rows // 3
+    side = (rows - whole) // 2
     me = lax.axis_index("cp")
     hd = lax.axis_index("hd")
     z = me // 4
@@ -38,8 +39,8 @@
         return zz * 4 + yy * 2 + xx
 
     piece_rows = {
-        "A": (0, third, 0), "B": (third, third, 1), "C": (2 * third, third, 2),
-        "C0": (2 * third, sixth, 2), "C1": (2 * third + sixth, sixth, 3),
+        "A": (0, side, 0), "B": (side, side, 1), "C": (2 * side, whole, 2),
+        "C0": (2 * side, whole // 2, 2), "C1": (2 * side + whole // 2, whole // 2, 3),
     }
 
     def part(src, piece):
@@ -182,11 +183,6 @@
     arrived(slot(z, *xn), "C")
     arrived(slot(z, *yn), "C")
     first_stage(go, [(yn, "C0")], [(xn, "C1")], [], 4, 4, 0)
-    arrived(slot(z, *xn), "B")
-    attend(slot(z, *xn))
-    arrived(slot(z, *yn), "A")
-    attend(slot(z, *yn))
-
     near = jnp.minimum(z, line - 1 - z)
 
     def plane(j):
@@ -199,7 +195,7 @@
         def _():
             fn(z - i, 0, has_up, up)
 
-        @pl.when(z + i < line)
+        @pl.when((z + i < line) & (i > 0))
         def _():
             fn(z + i, 1, has_down, down)
 
@@ -246,27 +242,35 @@
 
     dg_pieces = ("B", "A", "C0", "C1")
 
-    for piece in dg_pieces:
-        arrived(slot(z, *dg), piece)
-    attend(slot(z, *dg))
-
-    def stage(i, carry):
-        for n in range(3):
-            z_step(i, n, go)
+    def finish(i):
         here = plane(i)
-        attend(slot(here, *own))
+        for flips, pieces in ((xn, ("B",)), (yn, ("A",)), (dg, dg_pieces)):
+            wait_step(i, flips, pieces)
+            attend(slot(here, *flips))
+
+    def stage(i, carry, last=False):
+        z_step(i, 0, go)
+        z_step(i, 1, go)
+
+        @pl.when(i > 1)
+        def _():
+            corner_step(i - 1, go)
+
+        z_step(i, 2, go)
+        if last:
+            finish(i - 1)
+            attend(slot(plane(i), *own))
         z_step(i, 3, go)
         z_step(i, 4, go)
-        corner_step(i, go)
-        wait_step(i, xn, ("B",))
-        attend(slot(here, *xn))
-        wait_step(i, yn, ("A",))
-        attend(slot(here, *yn))
-        wait_step(i, dg, dg_pieces)
-        attend(slot(here, *dg))
+        if not last:
+            attend(slot(plane(i), *own))
+            finish(i - 1)
         return carry
 
-    lax.fori_loop(1, line, stage, 0)
+    lax.fori_loop(1, line - 1, stage, 0)
+    stage(line - 1, 0, last=True)
+    corner_step(line - 1, go)
+    finish(line - 1)
 
     for g in range(kv_heads):
         parts = [acc[g, c] / total[g, c] for c in range(tiles)]

time: 73.7 us -> 66.9 us (0.908)
  Pallas kernels: 71.5 us -> 64.7 us
    pallas_call x1, Pallas kernels: 71.5 us -> 64.7 us  [local(): pl.pallas_call(functools.partial(kernel, line), out_shape=jax.ShapeDtypeS...]
where the time goes in v3:
time: 66.9 us; the launch traced here: 66.8 us
  Pallas kernels  64.7 us (97%)
  local copies, waits for them, and re-layouts  2.06 us (3%)
    pallas_call x1, Pallas kernels, local(): pl.pallas_call(functools.partial(kernel, line), out_shape=jax.ShapeDtypeS...  64.7 us
    unnamed x1, local copies, waits for them, and re-layouts  2.06 us

profile of v3, /device:TPU:0, one launch (start us, length us, event | category | flops | bytes accessed | tf_op | source)
XLA Modules:
  0.0 66.8 jit_solution(5432208706918322097)
XLA Ops:
  0.0 64.7 %shard_map.64 = bf16[96,4096]{1,0:T(8,128)(2,1)} custom-call(bf16[192,2048]{1,0:T(8,128)(2,1)} %q_ref.1, s32[32]{0:T(128)} %span_ref.1, s32[24,128]{1,0:T(8,128)} %bitcast.1, bf16[192,512]{1,0:T(8,128)(2,1)} %k_hbm.1, bf16[192,512]{1,0:T(8,128)(2,1)} %v_hbm.1, bf16[2048,4096]{1,0:T(8,128)(2,1)} %w_hbm.1), custom_call_target="tpu_custom_call" | custom-call | tf_op jit(solution)/shard_map/pallas_call | solution.py:335
  64.7 2.1 %copy.8 = bf16[96,4096]{1,0:T(8,128)(2,1)} copy(bf16[96,4096]{1,0:T(8,128)(2,1)} %shard_map.64) | data formatting | bytes 1572864
